TPU v7x, 768 devices: a whole 4x8x12 slice. The times are simulated.
768 devices in a mesh: grp: 48 (over z, y_lo, core), shard: 16 (over y_hi, x).
Axes of the slice: x: 4, y: 8 (y_hi: 4, y_lo: 2; y = y_hi * 2 + y_lo), z: 12, core: 2. Of those that a mesh axis runs over, the one named last changes fastest.
Arguments:
- gradient: bfloat16 [48, 16, 384, 1024], P('grp', None, 'shard'), may hold values from -300 to 300
- momentum: float32 [48, 16, 384, 1024], P('grp', None, 'shard'), may hold values from -6 to 6
- owner: int32 [48, 16, 1], P('grp'), may hold values from 0 to 15; in each aligned block of 16 rows (0 to 15, 16 to 31, ..., all dimensions but the last counted through in order) at most 2 rows name the same one
Outputs:
- update: bfloat16 [48, 16, 384, 1024], P('grp', None, 'shard')
- momentum_out: float32 [48, 16, 384, 1024], P('grp', None, 'shard')
- slot_rms: float32 [48, 16, 2], P('grp', 'shard')
Inputs may be any that keep to these rules, and one draw needn't show every extreme that they name: `owner`: in every group no index of shard owns more than 2 matrices, and in some group some index owns exactly 2.
All inputs are finite; a program needn't handle non-finite values.
Results may differ from a plain program's by a relative error of at most 0.0085.
Values may be sent and summed in bfloat16 or wider, within the bound.
A program may use at most 32 MiB of HBM per device.

v0:
```python
import math

import jax
import jax.numpy as jnp
from jax import lax
from jax.sharding import Mesh
from jax.sharding import PartitionSpec as P

ITERS = 3
CAP = 2
SHARD = ("shard_0", "shard_1")
GRP = ("grp_0", "grp_1", "grp_2")
GRP_SHARD = ("grp_0", "grp_1", "grp_2", "shard_0", "shard_1")


QUINTIC_A = 3.4445
QUINTIC_B = -4.775
QUINTIC_C = 2.0315
MOMENTUM_DECAY = 0.95
CLIP_LEVEL = 0.5


def one_axis_at_a_time(array, axes):
    for axis in axes:
        array = lax.psum(array, axis)
    return array


def copy_for_each(array, axis):
    peers = lax.axis_size(axis)
    return lax.all_to_all(
        jnp.broadcast_to(array[None], (peers, *array.shape)), axis, 0, 0, tiled=True
    )


def of_everyone(array, axis):
    return copy_for_each(array, axis).sum(axis=0)


def newton_batch(matrices):
    wide = matrices.astype(jnp.float32)
    square_sum = jnp.sum(wide * wide, axis=(1, 2))
    iterate = (wide / (jnp.sqrt(square_sum) + 1e-07)[:, None, None]).astype(jnp.bfloat16)
    for repeat in range(ITERS):
        gram_matrix = jnp.einsum(
            "krc,ksc->krs", iterate, iterate, preferred_element_type=jnp.float32
        ).astype(jnp.bfloat16)
        squared = jnp.einsum(
            "krs,kst->krt", gram_matrix, gram_matrix, preferred_element_type=jnp.float32
        )
        blended = (QUINTIC_B * gram_matrix.astype(jnp.float32) + QUINTIC_C * squared).astype(
            jnp.bfloat16
        )
        product = jnp.einsum("krs,ksc->krc", blended, iterate, preferred_element_type=jnp.float32)
        iterate = (QUINTIC_A * iterate.astype(jnp.float32) + product).astype(jnp.bfloat16)
    return (iterate, square_sum)


def owner_tables(owners, shards, capacity):
    owner_hot = (owners[:, None] == jnp.arange(shards, dtype=jnp.int32)[None, :]).astype(jnp.int32)
    ranking = jnp.sum((jnp.cumsum(owner_hot, axis=0) - owner_hot) * owner_hot, axis=1)
    slot_hot = (ranking[:, None] == jnp.arange(capacity, dtype=jnp.int32)[None, :]).astype(
        jnp.int32
    )
    return (owner_hot, slot_hot)


def body(gradient, momentum, owner):
    shards = lax.axis_size(SHARD)
    matrices = gradient.shape[1]
    rows_dev = gradient.shape[2]
    columns = gradient.shape[3]
    full_rows = rows_dev * shards
    element_count = matrices * rows_dev * columns * shards * lax.axis_size(GRP)
    grad_wide = gradient.astype(jnp.float32)
    square_total = one_axis_at_a_time(jnp.sum(grad_wide * grad_wide), GRP_SHARD)
    clip_factor = jnp.minimum(
        jnp.float32(1.0), CLIP_LEVEL / jnp.sqrt(square_total / element_count + 1e-06)
    )
    momentum_out = MOMENTUM_DECAY * momentum + clip_factor * grad_wide
    nesterov = (clip_factor * grad_wide + MOMENTUM_DECAY * momentum_out).astype(jnp.bfloat16)[0]
    owners = owner[0, :, 0]
    owner_hot, slot_hot = owner_tables(owners, shards, CAP)
    blocks = nesterov.reshape(matrices // shards, shards, rows_dev, columns)
    ortho, square_sum = newton_batch(
        lax.all_to_all(blocks, SHARD, split_axis=1, concat_axis=2, tiled=True)[:, 0]
    )
    returned = lax.all_to_all(ortho[:, None], SHARD, split_axis=2, concat_axis=1, tiled=True)
    ortho_rows = returned.reshape(matrices, rows_dev, columns).astype(jnp.float32)
    local_wide = nesterov.astype(jnp.float32)
    matrix_squares = of_everyone(jnp.sum(local_wide * local_wide, axis=(1, 2)), SHARD)
    matrix_rms = jnp.sqrt(matrix_squares) / math.sqrt(full_rows * columns)
    myself = lax.axis_index(SHARD)
    mine = (owners == myself).astype(jnp.float32)
    slot_rms = jnp.sum(
        mine[:, None] * slot_hot.astype(jnp.float32) * matrix_rms[:, None], axis=0
    ).reshape(1, 1, CAP)
    update = (ortho_rows * math.sqrt(columns)).astype(jnp.bfloat16)[None]
    return (update, momentum_out, slot_rms)


def solution(mesh):
    finer = Mesh(
        mesh.devices.reshape(12, 2, 2, 4, 4), ("grp_0", "grp_1", "grp_2", "shard_0", "shard_1")
    )
    placed = (P(GRP, None, SHARD, None), P(GRP, None, SHARD, None), P(GRP, None, None))
    return jax.shard_map(
        body,
        mesh=finer,
        in_specs=placed,
        out_specs=(P(GRP, None, SHARD, None), P(GRP, None, SHARD, None), P(GRP, SHARD, None)),
        check_vma=False,
    )
```

profile of v0, /device:TPU:16, one launch (start us, length us, event | category | flops | bytes accessed | tf_op | source)
XLA Modules:
  0.0 147.4 jit_solution(3191149591708800997)
XLA Ops:
  0.6 2.1 %fusion.3 = f32[]{:T(128)} fusion(bf16[1,16,24,1024]{3,2,1,0:T(8,128)(2,1)} %param.3), kind=kLoop, calls=%fused_computation.7 | loop fusion | flops 1179647 | bytes 786436 | tf_op jit(solution)/shard_map/reduce_sum | solution.py:76
  2.8 33.9 %psum.35 = f32[]{:T(128)} all-reduce(f32[]{:T(128)} %fusion.3), channel_id=1, replica_groups=mesh['grp_0'=12,'grp_1'=2,'grp_2'=2,'shard_0'=4,'shard_1'=4] {'grp_0'}, use_global_device_ids=true, to_apply=%region_1.0 | all-reduce | flops 1 | bytes 8 | tf_op jit(solution)/shard_map/psum | solution.py:25
  36.7 5.5 %psum.36 = f32[]{:T(128)} all-reduce(f32[]{:T(128)} %psum.35), channel_id=1, replica_groups=mesh['grp_0'=12,'grp_1'=2,'grp_2'=2,'shard_0'=4,'shard_1'=4] {'grp_1'}, use_global_device_ids=true, to_apply=%region_2.0 | all-reduce | flops 1 | bytes 8 | tf_op jit(solution)/shard_map/psum | solution.py:25
  42.2 3.1 %psum.37 = f32[]{:T(128)} all-reduce(f32[]{:T(128)} %psum.36), channel_id=1, replica_groups=mesh['grp_0'=12,'grp_1'=2,'grp_2'=2,'shard_0'=4,'shard_1'=4] {'grp_2'}, use_global_device_ids=true, to_apply=%region_3.0 | all-reduce | flops 1 | bytes 8 | tf_op jit(solution)/shard_map/psum | solution.py:25
  45.3 11.8 %psum.38 = f32[]{:T(128)} all-reduce(f32[]{:T(128)} %psum.37), channel_id=1, replica_groups=mesh['grp_0'=12,'grp_1'=2,'grp_2'=2,'shard_0'=4,'shard_1'=4] {'shard_0'}, use_global_device_ids=true, to_apply=%region_4.0 | all-reduce | flops 1 | bytes 8 | tf_op jit(solution)/shard_map/psum | solution.py:25
  57.1 11.1 %psum.39 = f32[]{:T(128)} all-reduce(f32[]{:T(128)} %psum.38), channel_id=1, replica_groups=mesh['grp_0'=12,'grp_1'=2,'grp_2'=2,'shard_0'=4,'shard_1'=4] {'shard_1'}, use_global_device_ids=true, to_apply=%region_5.0 | all-reduce | flops 1 | bytes 8 | tf_op jit(solution)/shard_map/psum | solution.py:25
  68.9 3.2 %multiply_reduce_fusion = (f32[16]{0:T(128)S(1)}, bf16[1,16,24,1024]{3,2,0,1:T(8,128)(2,1)S(1)}, f32[1,16,24,1024]{3,2,1,0:T(8,128)}) fusion(f32[1,16,24,1024]{3,2,1,0:T(8,128)} %param.4, bf16[1,16,24,1024]{3,2,1,0:T(8,128)(2,1)} %param.3, f32[]{:T(128)S(6)} %min_shard_map.3), kind=kLoop, calls=%fused_computation.11 | loop fusion | flops 3932144 | bytes 4718660 | tf_op jit(solution)/shard_map/reduce_sum | solution.py:91
  72.1 23.2 %all_to_all.24 = bf16[1,16,24,1024]{3,2,0,1:T(8,128)(2,1)S(1)} all-to-all(bf16[1,16,24,1024]{3,2,0,1:T(8,128)(2,1)S(1)} %get-tuple-element.16), channel_id=1, replica_groups=mesh['grp_0'=12,'grp_1'=2,'grp_2'=2,'shard_0'=4,'shard_1'=4] {'shard_0',..., dimensions={1} | all-to-all | bytes 1572864 | tf_op jit(solution)/shard_map/all_to_all | solution.py:86
  95.3 0.6 broadcast_in_dim.5
  95.9 6.3 %all-to-all-start.2 = ((f32[16,1,16]{2,1,0:T(1,128)}), f32[16,1,16]{2,1,0:T(1,128)S(1)}, u32[]{:S(2)}, u32[]{:S(2)}) async-start(f32[16,1,16]{2,1,0:T(1,128)} %broadcast_in_dim.5), calls=%async_computation.2 | async-start | bytes 16384 | tf_op jit(solution)/shard_map/all_to_all | solution.py:31
  102.2 1.0 fusion.4
  103.9 0.2 fusion.5
  104.0 0.6 convolution_convert_fusion.2
  104.6 0.8 add_convert_fusion.2
  105.5 0.6 convolution_convert_fusion.1
  106.1 0.8 add_convert_fusion.1
  106.9 0.6 convolution_convert_fusion
  107.5 0.8 fusion.6
  108.3 1.2 copy.28
  109.5 0.5 broadcast.103
  110.0 5.2 %reduce.5 = bf16[384,1024]{1,0:T(8,128)(2,1)S(1)} reduce(bf16[384,1,1,1024]{3,2,1,0:T(2,128)(2,1)S(1)} %bitcast.43, bf16[]{:T(256)} %broadcast.103), dimensions={1,2}, to_apply=%bitcast.42.reduce_sub_computation | reduce | bytes 1572866
  115.3 0.0 copy-start
  115.3 1.4 reshape.167
  116.7 0.0 all-to-all-done.2
  116.7 9.6 %all-to-all-start.1 = ((bf16[16,2,12288]{2,1,0:T(2,128)(2,1)}), bf16[16,2,12288]{2,1,0:T(2,128)(2,1)S(1)}, u32[]{:S(2)}, u32[]{:S(2)}) async-start(bf16[16,2,12288]{2,1,0:T(2,128)(2,1)} %reshape.167), calls=%async_computation.1 | async-start | bytes 1572864 | tf_op jit(solution)/shard_map/all_to_all | solution.py:88
  126.3 0.0 copy-done
  126.3 0.1 fusion.26
  126.4 0.2 select_reduce_fusion
  126.7 0.6 fusion.30
  127.3 18.2 %all-to-all-done.1 = bf16[16,2,12288]{2,1,0:T(2,128)(2,1)S(1)} async-done(((bf16[16,2,12288]{2,1,0:T(2,128)(2,1)}), bf16[16,2,12288]{2,1,0:T(2,128)(2,1)S(1)}, u32[]{:S(2)}, u32[]{:S(2)}) %all-to-all-start.1) | async-done | bytes 786464 | tf_op jit(solution)/shard_map/all_to_all | solution.py:88
  145.5 0.7 reshape.168
  146.3 1.2 multiply_convert_fusion
  (4 shorter events, 0.1 us)
Async XLA Ops:
  95.9 20.8 %all-to-all-start.2 = ((f32[16,1,16]{2,1,0:T(1,128)}), f32[16,1,16]{2,1,0:T(1,128)S(1)}, u32[]{:S(2)}, u32[]{:S(2)}) async-start(f32[16,1,16]{2,1,0:T(1,128)} %broadcast_in_dim.5), calls=%async_computation.2 | async-start | bytes 16384 | tf_op jit(solution)/shard_map/all_to_all | solution.py:31
  115.3 11.0 %copy-start = (s32[1,16,1]{1,2,0:T(1,128)S(1)}, s32[1,16,1]{1,2,0:T(1,128)}, u32[]{:S(2)}) copy-start(s32[1,16,1]{1,2,0:T(1,128)} %param.5) | copy-start | bytes 196
  116.7 28.8 %all-to-all-start.1 = ((bf16[16,2,12288]{2,1,0:T(2,128)(2,1)}), bf16[16,2,12288]{2,1,0:T(2,128)(2,1)S(1)}, u32[]{:S(2)}, u32[]{:S(2)}) async-start(bf16[16,2,12288]{2,1,0:T(2,128)(2,1)} %reshape.167), calls=%async_computation.1 | async-start | bytes 1572864 | tf_op jit(solution)/shard_map/all_to_all | solution.py:88
where the time goes:
time: 148 us; the launch traced here: 147 us
  blocking collectives  88.6 us (60%)
  waiting for transfers between devices  18.2 us (12%)
  starting transfers between devices  15.9 us (11%)
  other arithmetic  13.9 us (9%)
  local copies, waits for them, and re-layouts  4.46 us (3%)
  matrix products  4.24 us (3%)
  between operations  2.11 us (1%)
    psum x5, blocking collectives, one_axis_at_a_time(): array = lax.psum(array, axis)  65.4 us
    all_to_all x1, blocking collectives, body(): lax.all_to_all(blocks, SHARD, split_axis=1, concat_axis=2, tiled=True)[:, 0]  23.2 us
    all_to_all x1, waiting for transfers between devices, body(): lax.all_to_all(ortho[:, None], SHARD, split_axis=2, concat_axis=1, tiled=...  18.2 us
    all_to_all x1, starting transfers between devices, body(): lax.all_to_all(ortho[:, None], SHARD, split_axis=2, concat_axis=1, tiled=...  9.63 us
    all_to_all x1, starting transfers between devices, copy_for_each(): lax.all_to_all(jnp.broadcast_to(array[None], (peers, *array.shape)), axis...  6.31 us
    unnamed x1, other arithmetic  5.24 us
    reduce_sum x1, other arithmetic, body(): jnp.sum(local_wide * local_wide, axis=(1, 2))  3.17 us
  transfers between devices with their start and end apart: 2, of which 1 were waited for; matrix products, arithmetic and copies ran while one was open for 10% of the time, Pallas kernels for 0%

commit v1 on v0

v1 whole, which is shorter than its diff:
```python
import functools
import math

import jax
import jax.numpy as jnp
from jax import lax
from jax.experimental import pallas as pl
from jax.experimental.pallas import tpu as pltpu
from jax.sharding import Mesh
from jax.sharding import PartitionSpec as P

ITERS = 3
CAP = 2
QUINTIC_A = 3.4445
QUINTIC_B = -4.775
QUINTIC_C = 2.0315
MOMENTUM_DECAY = 0.95
CLIP_LEVEL = 0.5

AXES = ("z", "yl", "c", "yh", "x")
SHARD = ("yh", "x")
GRP = ("z", "yl", "c")
LANES = 128


def displacements(yh_size, x_size):
    his = sorted(range(yh_size), key=lambda h: -min(2 * h + 1, 2 * (yh_size - h) - 1))
    return [(h, dx) for dx in range(x_size) for h in his]


def kernel(sizes, count, g_hbm, m_hbm, owner_ref, upd_ref, mom_ref, slot_ref,
           g_v, m_v, nest, got, mat, back, gram_v, part, p1, p2, p3, squares, square_row,
           load_sem, send_sem, recv_sem, back_send, back_recv, small_send, small_recv):
    z_size, yh_size, x_size = sizes
    mats, rows, cols = g_v.shape
    shards = yh_size * x_size
    z, yl, c = lax.axis_index("z"), lax.axis_index("yl"), lax.axis_index("c")
    yh, x = lax.axis_index("yh"), lax.axis_index("x")
    me = yh * x_size + x
    order = displacements(yh_size, x_size)

    def peer(k):
        h, dx = order[k]
        there_h = lax.rem(yh + h * (1 - yl) + (yh_size - h) * yl, yh_size)
        there_x = lax.rem(x + dx * (1 - yl) + (x_size - dx) * yl, x_size)
        return there_h, there_x

    def where(k):
        there_h, there_x = peer(k)
        return {"z": z, "yl": 1 - yl, "c": c, "yh": there_h, "x": there_x}

    def index(k):
        there_h, there_x = peer(k)
        return there_h * x_size + there_x

    quad = [{"z": z, "yl": lax.rem(yl + a, 2), "c": lax.rem(c + b, 2), "yh": yh, "x": x} for a, b in ((0, 1), (1, 0), (1, 1))]
    column = [{"z": lax.rem(z + k, z_size), "yl": yl, "c": c, "yh": yh, "x": x} for k in range(1, z_size)]

    half = mats // 2
    loads = []
    for part_at in range(2):
        span = pl.ds(part_at * half, half)
        loads.append(pltpu.make_async_copy(g_hbm.at[span], g_v.at[span], load_sem.at[part_at]))
    loads.append(pltpu.make_async_copy(m_hbm, m_v, load_sem.at[2]))
    for load in loads:
        load.start()

    barrier = pltpu.get_barrier_semaphore()
    for device in [quad[0], quad[2], *column]:
        pl.semaphore_signal(barrier, inc=1, device_id=device)
    for k in range(shards):
        pl.semaphore_signal(barrier, inc=1, device_id=where(k))

    def squared(first):
        def add(j, total):
            wide = g_v[first + j].astype(jnp.float32)
            return total + wide * wide
        return add

    total = jnp.zeros((rows, cols), jnp.float32)
    for part_at in range(2):
        loads[part_at].wait()
        total = lax.fori_loop(0, half, squared(part_at * half), total)
    part[0] = jnp.full((1, LANES), jnp.sum(total), jnp.float32)

    pl.semaphore_wait(barrier, 2 + len(column) + shards)

    def remote(source, target, sender, receiver, device):
        return pltpu.make_async_remote_copy(source, target, sender, receiver, device_id=device)

    for k, device in enumerate(quad):
        remote(part.at[0], p1.at[k], small_send.at[0], small_recv.at[0], device).start()
    remote(p1, p1, small_send.at[0], small_recv.at[0], quad[0]).wait()
    part[1] = part[0] + jnp.sum(p1[...], axis=0)
    for k, device in enumerate(column):
        remote(part.at[1], p2.at[k], small_send.at[1], small_recv.at[1], device).start()
    remote(p2, p2, small_send.at[1], small_recv.at[1], column[0]).wait()
    part[2] = part[1] + jnp.sum(p2[...], axis=0)
    for k in range(shards):
        remote(part.at[2], p3.at[k], small_send.at[2], small_recv.at[2], where(k)).start()
    loads[2].wait()
    remote(p3, p3, small_send.at[2], small_recv.at[2], where(0)).wait()

    mean = jnp.sum(p3[...], axis=0) / count
    clip = jnp.max(jnp.minimum(1.0, CLIP_LEVEL / jnp.sqrt(mean + 1e-06)))

    for k in range(shards):
        j = index(k)
        pulled = clip * g_v[j].astype(jnp.float32)
        kept = MOMENTUM_DECAY * m_v[j] + pulled
        m_v[j] = kept
        nest[k] = (pulled + MOMENTUM_DECAY * kept).astype(jnp.bfloat16)
        remote(nest.at[k], got.at[k], send_sem, recv_sem.at[k], where(k)).start()
    mom_copy = pltpu.make_async_copy(m_v, mom_ref, load_sem.at[3])
    mom_copy.start()

    total = jnp.zeros((rows, cols), jnp.float32)
    for k in range(shards):
        remote(nest.at[k], got.at[k], send_sem, recv_sem.at[k], where(k)).wait_recv()
        wide = got[k].astype(jnp.float32)
        total = total + wide * wide
    square_sum = jnp.sum(total)
    norm = jnp.sqrt(jnp.full((1, LANES), square_sum, jnp.float32))
    scale = jnp.max(1.0 / (norm + 1e-07))
    square_row[...] = norm
    for k in range(shards):
        remote(square_row, squares.at[k], small_send.at[3], small_recv.at[3], where(k)).start()
    for k in range(0, shards, 2):
        pair = jnp.concatenate([got[k].astype(jnp.float32), got[k + 1].astype(jnp.float32)], axis=0)
        mat[pl.ds(k * rows, 2 * rows), :] = (pair * scale).astype(jnp.bfloat16)

    over = (((1,), (1,)), ((), ()))
    plain = (((1,), (0,)), ((), ()))
    full = shards * rows
    for repeat in range(ITERS):
        iterate = mat[...]
        gram_v[...] = lax.dot_general(iterate, iterate, over, preferred_element_type=jnp.float32).astype(jnp.bfloat16)
        gram = gram_v[...]
        squared_gram = lax.dot_general(gram, gram, plain, preferred_element_type=jnp.float32)
        gram_v[...] = (QUINTIC_B * gram.astype(jnp.float32) + QUINTIC_C * squared_gram).astype(jnp.bfloat16)
        if repeat < ITERS - 1:
            product = lax.dot_general(gram_v[...], iterate, plain, preferred_element_type=jnp.float32)
            mat[...] = (QUINTIC_A * iterate.astype(jnp.float32) + product).astype(jnp.bfloat16)

    chunk = 4 if shards % 4 == 0 else 2
    for first in range(0, shards, chunk):
        span = pl.ds(first * rows, chunk * rows)
        product = lax.dot_general(gram_v[span, :], mat[...], plain, preferred_element_type=jnp.float32)
        final = (QUINTIC_A * mat[span, :].astype(jnp.float32) + product) * math.sqrt(cols)
        for k in range(first, first + chunk):
            back[k] = final[(k - first) * rows:(k - first + 1) * rows].astype(jnp.bfloat16)
            remote(back.at[k], upd_ref.at[me], back_send, back_recv, where(k)).start()

    remote(squares, squares, small_send.at[3], small_recv.at[3], where(0)).wait()
    taken = jnp.int32(0)
    slots = [jnp.zeros((1, LANES), jnp.float32) for _ in range(CAP)]
    rms = [squares[k] / math.sqrt(full * cols) for k in range(shards)]
    named = [(index(k), rms[k]) for k in range(shards)]
    for j in range(mats):
        mine = (owner_ref[0, j] == me).astype(jnp.int32)
        rank = taken
        taken = taken + mine
        for s in range(CAP):
            hit = mine * (rank == s).astype(jnp.int32)
            for place, value in named:
                slots[s] = slots[s] + (hit * (place == j).astype(jnp.int32)).astype(jnp.float32) * value
    lane = lax.broadcasted_iota(jnp.int32, (1, LANES), 1)
    slot_ref[...] = jnp.where(lane == 0, slots[0], slots[1])

    remote(nest, got, send_sem, recv_sem.at[0], where(0)).wait_send()
    mom_copy.wait()
    remote(upd_ref, upd_ref, back_send, back_recv, where(0)).wait()


def body(gradient, momentum, owner):
    sizes = (lax.axis_size("z"), lax.axis_size("yh"), lax.axis_size("x"))
    shards = sizes[1] * sizes[2]
    _, mats, rows, cols = gradient.shape
    count = mats * rows * cols * shards * lax.axis_size(GRP)
    full = rows * shards
    anywhere, vmem = pl.BlockSpec(memory_space=pl.ANY), pl.BlockSpec(memory_space=pltpu.VMEM)
    dma = pltpu.SemaphoreType.DMA
    update, momentum_out, slots = pl.pallas_call(
        functools.partial(kernel, sizes, count),
        name="muon",
        out_shape=(
            jax.ShapeDtypeStruct((mats, rows, cols), jnp.bfloat16),
            jax.ShapeDtypeStruct((mats, rows, cols), jnp.float32),
            jax.ShapeDtypeStruct((1, LANES), jnp.float32),
        ),
        in_specs=[anywhere, anywhere, pl.BlockSpec(memory_space=pltpu.SMEM)],
        out_specs=(vmem, anywhere, vmem),
        scratch_shapes=[
            pltpu.VMEM((mats, rows, cols), jnp.bfloat16),
            pltpu.VMEM((mats, rows, cols), jnp.float32),
            pltpu.VMEM((shards, rows, cols), jnp.bfloat16),
            pltpu.VMEM((shards, rows, cols), jnp.bfloat16),
            pltpu.VMEM((full, cols), jnp.bfloat16),
            pltpu.VMEM((shards, rows, cols), jnp.bfloat16),
            pltpu.VMEM((full, full), jnp.bfloat16),
            pltpu.VMEM((3, 1, LANES), jnp.float32),
            pltpu.VMEM((3, 1, LANES), jnp.float32),
            pltpu.VMEM((sizes[0] - 1, 1, LANES), jnp.float32),
            pltpu.VMEM((shards, 1, LANES), jnp.float32),
            pltpu.VMEM((shards, 1, LANES), jnp.float32),
            pltpu.VMEM((1, LANES), jnp.float32),
            dma((4,)),
            dma,
            dma((shards,)),
            dma,
            dma,
            dma((4,)),
            dma((4,)),
        ],
        compiler_params=pltpu.CompilerParams(collective_id=0, has_side_effects=True),
    )(gradient[0], momentum[0], owner.reshape(1, mats))
    return update[None], momentum_out[None], slots[:, None, :CAP]


def solution(mesh):
    finer = Mesh(mesh.devices.reshape(12, 2, 2, 4, 4), AXES)
    return jax.shard_map(
        body,
        mesh=finer,
        in_specs=(P(GRP, None, SHARD, None), P(GRP, None, SHARD, None), P(GRP, None, None)),
        out_specs=(P(GRP, None, SHARD, None), P(GRP, None, SHARD, None), P(GRP, SHARD, None)),
        check_vma=False,
    )
```

time: 148 us -> 80.4 us (0.54)
  the two profiles are of different devices: /device:TPU:16 before, /device:TPU:1 now
where the time goes in v1:
time: 80.4 us; the launch traced here: 79.5 us
  Pallas kernels  74.3 us (92%)
  local copies, waits for them, and re-layouts  4.52 us (6%)
    pallas_call x1, Pallas kernels, body(): pl.pallas_call(functools.partial(kernel, sizes, count), name='muon', out_...  74.3 us
    unnamed x4, local copies, waits for them, and re-layouts  3.21 us

profile of v1, /device:TPU:1, one launch (start us, length us, event | category | flops | bytes accessed | tf_op | source)
XLA Modules:
  0.0 79.5 jit_solution(12566401125008389969)
XLA Ops:
  0.6 74.3 %muon.1 = (bf16[16,24,1024]{2,1,0:T(8,128)(2,1)}, f32[16,24,1024]{2,1,0:T(8,128)}, f32[1,128]{1,0:T(1,128)}) custom-call(bf16[16,24,1024]{2,1,0:T(8,128)(2,1)} %bitcast.9, f32[16,24,1024]{2,1,0:T(8,128)} %bitcast.7, s32[1,16]{1,0:T(1,128)} %bitcast.11), custom_call_target="tpu_custom_call" | custom-call | tf_op jit(solution)/shard_map/muon/pallas_call | solution.py:183
  75.0 0.0 copy-start
  75.0 1.3 %slice_bitcast_fusion = f32[1,1,2]{2,1,0:T(1,128)} fusion(f32[1,128]{1,0:T(1,128)} %get-tuple-element.8), kind=kLoop, calls=%fused_computation | loop fusion | bytes 16 | tf_op jit(solution)/shard_map/broadcast_in_dim | solution.py:217
  76.3 2.1 %copy.8 = bf16[1,16,24,1024]{3,2,1,0:T(8,128)(2,1)} copy(bf16[1,16,24,1024]{3,2,1,0:T(8,128)(2,1)} %bitcast.10) | data formatting | bytes 1572864
  78.4 0.0 copy-done
  78.4 1.1 %copy.9 = f32[1,16,24,1024]{3,2,1,0:T(8,128)} copy(f32[1,16,24,1024]{3,2,1,0:T(8,128)S(1)} %bitcast.8) | data formatting | bytes 3145728
Async XLA Ops:
  75.0 3.4 %copy-start = (f32[16,24,1024]{2,1,0:T(8,128)S(1)}, f32[16,24,1024]{2,1,0:T(8,128)}, u32[]{:S(2)}) copy-start(f32[16,24,1024]{2,1,0:T(8,128)} %get-tuple-element.7) | copy-start | bytes 4718596

commit v2 on v1

v2 whole, which is shorter than its diff:
```python
import functools
import math

import jax
import jax.numpy as jnp
from jax import lax
from jax.experimental import pallas as pl
from jax.experimental.pallas import tpu as pltpu
from jax.sharding import Mesh
from jax.sharding import PartitionSpec as P

ITERS = 3
CAP = 2
QUINTIC_A = 3.4445
QUINTIC_B = -4.775
QUINTIC_C = 2.0315
MOMENTUM_DECAY = 0.95
CLIP_LEVEL = 0.5

AXES = ("z", "yl", "c", "yh", "x")
SHARD = ("yh", "x")
GRP = ("z", "yl", "c")
LANES = 128


def early_blocks(z, c, shards):
    return (1 - c) * (shards - shards // 4 * (1 - lax.div(16 - z, 12)))


def kernel(sizes, count, g_hbm, m_hbm, owner_hbm, upd_ref, mom_ref, slot_ref,
           owner_ref, pair_v, m_v, got_pair, nest, got, mat, back, gram_v, part, p1, p2, p3, whole, squares, square_row,
           g_sem, load_sem, send_sem, pair_recv, recv_sem, back_send, back_recv, small_send, small_recv):
    z_size, yh_size, x_size = sizes
    mats, rows, cols = m_v.shape
    shards = yh_size * x_size
    z, yl, c = lax.axis_index("z"), lax.axis_index("yl"), lax.axis_index("c")
    yh, x = lax.axis_index("yh"), lax.axis_index("x")
    me = yh * x_size + x
    early = early_blocks(z, c, shards)
    turn = me + 2 * yl

    def peer(k):
        h, dx = lax.rem(k + 1, yh_size), lax.div(k, yh_size)
        there_h = lax.rem(yh + h * (1 - yl) + (yh_size - h) * yl, yh_size)
        there_x = lax.rem(x + dx * (1 - yl) + (x_size - dx) * yl, x_size)
        return there_h, there_x

    def where(k):
        there_h, there_x = peer(jnp.int32(k))
        return {"z": z, "yl": 1 - yl, "c": c, "yh": there_h, "x": there_x}

    def index(k):
        there_h, there_x = peer(jnp.int32(k))
        return there_h * x_size + there_x

    def remote(source, target, sender, receiver, device):
        return pltpu.make_async_remote_copy(source, target, sender, receiver, device_id=device)

    here = {"z": z, "yl": yl, "c": c, "yh": yh, "x": x}
    other_core = {**here, "c": 1 - c}
    far_first = sorted(range(1, z_size), key=lambda k: -min(k, z_size - k))
    column = {k: {**here, "z": lax.rem(z + k, z_size)} for k in far_first}
    same_lo = {k: {**here, "yh": lax.rem(yh + k // x_size, yh_size), "x": lax.rem(x + k % x_size, x_size)} for k in range(1, shards)}

    barrier = pltpu.get_barrier_semaphore()

    @pl.when(c == 1)
    def _():
        for device in (*column.values(), *same_lo.values()):
            pl.semaphore_signal(barrier, inc=1, device_id=device)

    for k in range(shards):
        pl.semaphore_signal(barrier, inc=1, device_id=where(k))
    pl.semaphore_signal(barrier, inc=1, device_id=other_core)

    def g_load(k):
        return pltpu.make_async_copy(g_hbm.at[index(k)], pair_v.at[k, 0], g_sem.at[k])

    for k in range(shards):
        g_load(k).start()
    m_load = pltpu.make_async_copy(m_hbm, m_v, load_sem.at[0])
    m_load.start()
    owner_load = pltpu.make_async_copy(owner_hbm, owner_ref, load_sem.at[1])
    owner_load.start()

    def add_gradient(k, total):
        g_load(k).wait()
        wide = pair_v[k, 0].astype(jnp.float32)
        return total + wide * wide

    nothing = jnp.zeros((rows, cols), jnp.float32)
    part[0] = jnp.full((1, LANES), jnp.sum(lax.fori_loop(0, shards, add_gradient, nothing)), jnp.float32)

    pl.semaphore_wait(barrier, 1 + shards + c * (len(column) + len(same_lo)))

    def part_copy():
        return remote(part.at[0], p1.at[0], small_send.at[0], small_recv.at[0], other_core)

    def sum_copy():
        return remote(whole.at[0], whole.at[0], small_send.at[4], small_recv.at[4], other_core)

    @pl.when(c == 0)
    def _():
        part_copy().start()

    m_load.wait()

    def send_pair(i, _):
        k = lax.rem(i + turn, early)
        pair_v[k, 1] = m_v[index(k)].astype(jnp.bfloat16)
        remote(pair_v.at[k], got_pair.at[k], send_sem.at[k], pair_recv.at[k], where(k)).start()
        return 0

    lax.fori_loop(0, early, send_pair, 0)

    @pl.when(c == 0)
    def _():
        part_copy().wait_send()
        sum_copy().wait_recv()

    @pl.when(c == 1)
    def _():
        part_copy().wait_recv()
        part[1] = part[0] + p1[0]
        for k, device in same_lo.items():
            remote(part.at[1], p3.at[shards + k - 1], small_send.at[1], small_recv.at[1], device).start()
        for k in range(shards):
            remote(part.at[1], p3.at[k], small_send.at[1], small_recv.at[1], where(k)).start()
        remote(p3, p3, small_send.at[1], small_recv.at[1], where(0)).wait()
        part[2] = part[1] + jnp.sum(p3[...], axis=0)
        for k, device in column.items():
            remote(part.at[2], p2.at[k - 1], small_send.at[2], small_recv.at[2], device).start()
        remote(p2, p2, small_send.at[2], small_recv.at[2], column[1]).wait()
        whole[0] = part[2] + jnp.sum(p2[...], axis=0)
        sum_copy().start()

    mean = whole[0] / count
    clip = jnp.max(jnp.minimum(1.0, CLIP_LEVEL / jnp.sqrt(mean + 1e-06)))

    def nesterov_of(gradient, momentum):
        pulled = clip * gradient.astype(jnp.float32)
        return (pulled + MOMENTUM_DECAY * (MOMENTUM_DECAY * momentum.astype(jnp.float32) + pulled)).astype(jnp.bfloat16)

    def nesterov_copy(i):
        k = early + lax.rem(i + turn, shards - early)
        return k, remote(nest.at[k], got.at[k], send_sem.at[k], recv_sem.at[k], where(k))

    def send_nesterov(i, _):
        k, copy = nesterov_copy(i)
        nest[k] = nesterov_of(pair_v[k, 0], m_v[index(k)])
        copy.start()
        return 0

    lax.fori_loop(0, shards - early, send_nesterov, 0)

    def add_pair(k, total):
        remote(pair_v.at[k], got_pair.at[k], send_sem.at[k], pair_recv.at[k], where(k)).wait_recv()
        block = nesterov_of(got_pair[k, 0], got_pair[k, 1])
        got[k] = block
        wide = block.astype(jnp.float32)
        return total + wide * wide

    def add_nesterov(k, total):
        remote(nest.at[k], got.at[k], send_sem.at[k], recv_sem.at[k], where(k)).wait_recv()
        wide = got[k].astype(jnp.float32)
        return total + wide * wide

    total = lax.fori_loop(early, shards, add_nesterov, lax.fori_loop(0, early, add_pair, nothing))

    norm = jnp.sqrt(jnp.full((1, LANES), jnp.sum(total), jnp.float32))
    scale = jnp.max(1.0 / (norm + 1e-07))
    square_row[...] = norm
    for k in range(shards):
        remote(square_row, squares.at[k], small_send.at[3], small_recv.at[3], where(k)).start()
    for k in range(0, shards, 2):
        pair = jnp.concatenate([got[k].astype(jnp.float32), got[k + 1].astype(jnp.float32)], axis=0)
        mat[pl.ds(k * rows, 2 * rows), :] = (pair * scale).astype(jnp.bfloat16)

    over = (((1,), (1,)), ((), ()))
    plain = (((1,), (0,)), ((), ()))
    full = shards * rows
    for repeat in range(ITERS):
        iterate = mat[...]
        gram_v[...] = lax.dot_general(iterate, iterate, over, preferred_element_type=jnp.float32).astype(jnp.bfloat16)
        gram = gram_v[...]
        squared_gram = lax.dot_general(gram, gram, plain, preferred_element_type=jnp.float32)
        gram_v[...] = (QUINTIC_B * gram.astype(jnp.float32) + QUINTIC_C * squared_gram).astype(jnp.bfloat16)
        if repeat < ITERS - 1:
            product = lax.dot_general(gram_v[...], iterate, plain, preferred_element_type=jnp.float32)
            mat[...] = (QUINTIC_A * iterate.astype(jnp.float32) + product).astype(jnp.bfloat16)

    chunk = 4 if shards % 4 == 0 else 2
    for i in range(shards // chunk):
        first = lax.rem(i + turn, shards // chunk) * chunk
        span = pl.ds(pl.multiple_of(first * rows, chunk * rows), chunk * rows)
        product = lax.dot_general(gram_v[span, :], mat[...], plain, preferred_element_type=jnp.float32)
        final = (QUINTIC_A * mat[span, :].astype(jnp.float32) + product) * math.sqrt(cols)
        for k in range(chunk):
            back[first + k] = final[k * rows:(k + 1) * rows].astype(jnp.bfloat16)
            remote(back.at[first + k], upd_ref.at[me], back_send, back_recv, where(first + k)).start()

    def keep(k, _):
        j = index(k)
        mom_ref[j] = MOMENTUM_DECAY * m_v[j] + clip * pair_v[k, 0].astype(jnp.float32)
        return 0

    lax.fori_loop(0, shards, keep, 0)

    remote(squares, squares, small_send.at[3], small_recv.at[3], where(0)).wait()
    owner_load.wait()
    taken = jnp.int32(0)
    slots = [jnp.zeros((1, LANES), jnp.float32) for _ in range(CAP)]
    named = [(index(k), squares[k] / math.sqrt(full * cols)) for k in range(shards)]
    for j in range(mats):
        mine = (owner_ref[0, j] == me).astype(jnp.int32)
        rank = taken
        taken = taken + mine
        for s in range(CAP):
            hit = mine * (rank == s).astype(jnp.int32)
            for place, value in named:
                slots[s] = slots[s] + (hit * (place == j).astype(jnp.int32)).astype(jnp.float32) * value
    lane = lax.broadcasted_iota(jnp.int32, (1, LANES), 1)
    slot_ref[0] = jnp.where(lane == 0, slots[0], slots[1])[:, :CAP]

    def pair_left(k, _):
        remote(pair_v.at[k], got_pair.at[k], send_sem.at[k], pair_recv.at[k], where(k)).wait_send()
        return 0

    def nesterov_left(i, _):
        nesterov_copy(i)[1].wait_send()
        return 0

    lax.fori_loop(0, early, pair_left, 0)
    lax.fori_loop(0, shards - early, nesterov_left, 0)

    @pl.when(c == 1)
    def _():
        sum_copy().wait_send()

    remote(upd_ref, upd_ref, back_send, back_recv, where(0)).wait()


def finish(*refs):
    sources, targets, sem = refs[:3], refs[3:6], refs[6]
    copies = [pltpu.make_async_copy(a, b, sem.at[i]) for i, (a, b) in enumerate(zip(sources, targets))]
    for copy in copies:
        copy.start()
    for copy in copies:
        copy.wait()


def body(gradient, momentum, owner):
    sizes = (lax.axis_size("z"), lax.axis_size("yh"), lax.axis_size("x"))
    shards = sizes[1] * sizes[2]
    _, mats, rows, cols = gradient.shape
    count = mats * rows * cols * shards * lax.axis_size(GRP)
    full = rows * shards
    far, vmem = pl.BlockSpec(memory_space=pltpu.HBM), pl.BlockSpec(memory_space=pltpu.VMEM)
    dma = pltpu.SemaphoreType.DMA
    arguments = (gradient[0], momentum[0], owner.reshape(1, mats))
    results = pl.pallas_call(
        functools.partial(kernel, sizes, count),
        name="muon",
        out_shape=(
            pltpu.VMEM((mats, rows, cols), jnp.bfloat16),
            pltpu.VMEM((mats, rows, cols), jnp.float32),
            pltpu.VMEM((1, 1, CAP), jnp.float32),
        ),
        in_specs=[far] * 3,
        out_specs=(vmem,) * 3,
        scratch_shapes=[
            pltpu.SMEM((1, mats), jnp.int32),
            pltpu.VMEM((shards, 2, rows, cols), jnp.bfloat16),
            pltpu.VMEM((mats, rows, cols), jnp.float32),
            pltpu.VMEM((shards, 2, rows, cols), jnp.bfloat16),
            pltpu.VMEM((shards, rows, cols), jnp.bfloat16),
            pltpu.VMEM((shards, rows, cols), jnp.bfloat16),
            pltpu.VMEM((full, cols), jnp.bfloat16),
            pltpu.VMEM((shards, rows, cols), jnp.bfloat16),
            pltpu.VMEM((full, full), jnp.bfloat16),
            pltpu.VMEM((3, 1, LANES), jnp.float32),
            pltpu.VMEM((1, 1, LANES), jnp.float32),
            pltpu.VMEM((sizes[0] - 1, 1, LANES), jnp.float32),
            pltpu.VMEM((2 * shards - 1, 1, LANES), jnp.float32),
            pltpu.VMEM((1, 1, LANES), jnp.float32),
            pltpu.VMEM((shards, 1, LANES), jnp.float32),
            pltpu.VMEM((1, LANES), jnp.float32),
            dma((shards,)),
            dma((2,)),
            dma((shards,)),
            dma((shards,)),
            dma((shards,)),
            dma,
            dma,
            dma((5,)),
            dma((5,)),
        ],
        compiler_params=pltpu.CompilerParams(collective_id=0, has_side_effects=True, vmem_limit_bytes=24 << 20),
    )(*(pltpu.with_memory_space_constraint(a, pltpu.HBM) for a in arguments))
    update, momentum_out, slots = pl.pallas_call(
        finish,
        name="finish",
        out_shape=tuple(jax.ShapeDtypeStruct(a.shape, a.dtype) for a in results),
        in_specs=[vmem] * 3,
        out_specs=(far,) * 3,
        scratch_shapes=[dma((3,))],
        compiler_params=pltpu.CompilerParams(vmem_limit_bytes=8 << 20),
    )(*results)
    return update[None], momentum_out[None], slots


def solution(mesh):
    finer = Mesh(mesh.devices.reshape(12, 2, 2, 4, 4), AXES)
    return jax.shard_map(
        body,
        mesh=finer,
        in_specs=(P(GRP, None, SHARD, None), P(GRP, None, SHARD, None), P(GRP, None, None)),
        out_specs=(P(GRP, None, SHARD, None), P(GRP, None, SHARD, None), P(GRP, SHARD, None)),
        check_vma=False,
    )
```

time: 80.4 us -> 62.3 us (0.77)
  Pallas kernels: 74.3 us -> 61 us
  local copies, waits for them, and re-layouts: 4.52 us -> 0 us
    pallas_call x1, Pallas kernels: 74.3 us -> 59.6 us  [body(): pl.pallas_call(functools.partial(kernel, sizes, count), name='muon', out_...]
    unnamed x4 -> x0, local copies, waits for them, and re-layouts: 3.21 us -> none
    pallas_call x0 -> x1, Pallas kernels: none -> 1.43 us  [body(): pl.pallas_call(finish, name='finish', out_shape=tuple((jax.ShapeDtypeStru...]
    broadcast_in_dim x1 -> x0, local copies, waits for them, and re-layouts: 1.31 us -> none  [body(): return (update[None], momentum_out[None], slots[:, None, :CAP])]
where the time goes in v2:
time: 62.3 us; the launch traced here: 61.7 us
  Pallas kernels  61 us (98%)
  between operations  0.64 us (1%)
    pallas_call x1, Pallas kernels, body(): pl.pallas_call(functools.partial(kernel, sizes, count), name='muon', out_...  59.6 us
    pallas_call x1, Pallas kernels, body(): pl.pallas_call(finish, name='finish', out_shape=tuple((jax.ShapeDtypeStru...  1.43 us

profile of v2, /device:TPU:1, one launch (start us, length us, event | category | flops | bytes accessed | tf_op | source)
XLA Modules:
  0.0 61.7 jit_solution(7266252810612443565)
XLA Ops:
  0.6 59.6 %muon.1 = (bf16[16,24,1024]{2,1,0:T(8,128)(2,1)S(1)}, f32[16,24,1024]{2,1,0:T(8,128)S(1)}, f32[1,1,2]{2,1,0:T(1,128)S(1)}) custom-call(bf16[16,24,1024]{2,1,0:T(8,128)(2,1)} %bitcast.6, f32[16,24,1024]{2,1,0:T(8,128)} %bitcast.5, s32[1,16]{1,0:T(1,128)} %bitcast.7), custom_call_target="tpu_custom_call" | custom-call | tf_op jit(solution)/shard_map/muon/pallas_call | solution.py:261
  60.2 1.4 %finish.1 = (bf16[16,24,1024]{2,1,0:T(8,128)(2,1)}, f32[16,24,1024]{2,1,0:T(8,128)}, f32[1,1,2]{2,1,0:T(1,128)}) custom-call(bf16[16,24,1024]{2,1,0:T(8,128)(2,1)S(1)} %get-tuple-element.9.refs_0_, f32[16,24,1024]{2,1,0:T(8,128)S(1)} %get-tuple-element.10.refs_1_, f32[1,1,2]{2,1,0:T(1,128)S(1)} %get-tuple-element.11.refs_2_), custom_call_target="tpu_custom_call" | custom-call | tf_op jit(solution)/shard_map/finish/pallas_call | solution.py:300

commit v3 on v2

--- a/solution.py
+++ b/solution.py
@@ -21,23 +21,37 @@
 SHARD = ("yh", "x")
 GRP = ("z", "yl", "c")
 LANES = 128
-
-
-def early_blocks(z, c, shards):
-    return (1 - c) * (shards - shards // 4 * (1 - lax.div(16 - z, 12)))
+ALL_UP_TO = 4
+LATE_TAIL = 4
+HOLD = 2
+
+
+def up_to(z, last):
+    return lax.div(12 + last - z, 12)
+
+
+def early_blocks(z, shards):
+    return shards - shards // LATE_TAIL * (1 - up_to(z, ALL_UP_TO))
 
 
 def kernel(sizes, count, g_hbm, m_hbm, owner_hbm, upd_ref, mom_ref, slot_ref,
            owner_ref, pair_v, m_v, got_pair, nest, got, mat, back, gram_v, part, p1, p2, p3, whole, squares, square_row,
-           g_sem, load_sem, send_sem, pair_recv, recv_sem, back_send, back_recv, small_send, small_recv):
+           g_sem, load_sem, send_sem, pair_recv, recv_sem, back_send, back_recv, small_send, small_recv, go_sem, late_sem, column_sem, ready_sem):
     z_size, yh_size, x_size = sizes
     mats, rows, cols = m_v.shape
     shards = yh_size * x_size
     z, yl, c = lax.axis_index("z"), lax.axis_index("yl"), lax.axis_index("c")
     yh, x = lax.axis_index("yh"), lax.axis_index("x")
     me = yh * x_size + x
-    early = early_blocks(z, c, shards)
+    tail = shards - early_blocks(z, shards)
+    early = (1 - c) * (shards - tail)
     turn = me + 2 * yl
+    late = (z + yl + c + me == 0).astype(jnp.int32)
+    beside_late = (z + (1 - yl) == 0).astype(jnp.int32)
+    meets_late = beside_late * (1 - c)
+    its_place = x * yh_size + lax.rem(yh + yh_size - 1, yh_size)
+    its_time = shards // 2 + lax.rem(me, shards // 2)
+    pair_turn = meets_late * (its_place + shards - its_time) + (1 - meets_late) * turn
 
     def peer(k):
         h, dx = lax.rem(k + 1, yh_size), lax.div(k, yh_size)
@@ -66,11 +80,19 @@
 
     @pl.when(c == 1)
     def _():
-        for device in (*column.values(), *same_lo.values()):
+        for device in same_lo.values():
             pl.semaphore_signal(barrier, inc=1, device_id=device)
-
-    for k in range(shards):
-        pl.semaphore_signal(barrier, inc=1, device_id=where(k))
+        for k, device in column.items():
+
+            @pl.when(z + k < z_size)
+            def _():
+                pl.semaphore_signal(barrier, inc=1, device_id=device)
+
+    @pl.when(late == 0)
+    def _():
+        for k in range(shards):
+            pl.semaphore_signal(barrier, inc=1, device_id={**where(k), "c": 1})
+
     pl.semaphore_signal(barrier, inc=1, device_id=other_core)
 
     def g_load(k):
@@ -91,7 +113,7 @@
     nothing = jnp.zeros((rows, cols), jnp.float32)
     part[0] = jnp.full((1, LANES), jnp.sum(lax.fori_loop(0, shards, add_gradient, nothing)), jnp.float32)
 
-    pl.semaphore_wait(barrier, 1 + shards + c * (len(column) + len(same_lo)))
+    pl.semaphore_wait(barrier, 1 + c * (2 * shards - beside_late + z + len(same_lo)))
 
     def part_copy():
         return remote(part.at[0], p1.at[0], small_send.at[0], small_recv.at[0], other_core)
@@ -102,32 +124,58 @@
     @pl.when(c == 0)
     def _():
         part_copy().start()
-
-    m_load.wait()
-
-    def send_pair(i, _):
-        k = lax.rem(i + turn, early)
-        pair_v[k, 1] = m_v[index(k)].astype(jnp.bfloat16)
-        remote(pair_v.at[k], got_pair.at[k], send_sem.at[k], pair_recv.at[k], where(k)).start()
-        return 0
-
-    lax.fori_loop(0, early, send_pair, 0)
-
-    @pl.when(c == 0)
-    def _():
-        part_copy().wait_send()
-        sum_copy().wait_recv()
+        pl.semaphore_wait(ready_sem, 1)
+
+        @pl.when(late == 1)
+        def _():
+            for k in range(shards):
+                pl.semaphore_signal(late_sem, inc=1, device_id=where(k))
 
     @pl.when(c == 1)
     def _():
+        pl.semaphore_signal(ready_sem, inc=1, device_id=other_core)
         part_copy().wait_recv()
         part[1] = part[0] + p1[0]
         for k, device in same_lo.items():
             remote(part.at[1], p3.at[shards + k - 1], small_send.at[1], small_recv.at[1], device).start()
         for k in range(shards):
             remote(part.at[1], p3.at[k], small_send.at[1], small_recv.at[1], where(k)).start()
+        for k, device in column.items():
+
+            @pl.when(z + k >= z_size)
+            def _():
+                pl.semaphore_signal(column_sem, inc=1, device_id=device)
+
+    m_load.wait()
+
+    def send_pair(i, _):
+        k = lax.rem(i + pair_turn, early)
+        pair_v[k, 1] = m_v[index(k)].astype(jnp.bfloat16)
+        remote(pair_v.at[k], got_pair.at[k], send_sem.at[k], pair_recv.at[k], where(k)).start()
+        return 0
+
+    lax.fori_loop(0, lax.div(early, 2), send_pair, 0)
+
+    @pl.when(meets_late == 1)
+    def _():
+        pl.semaphore_wait(late_sem, 1)
+
+    lax.fori_loop(lax.div(early, 2), early, send_pair, 0)
+
+    @pl.when(c == 0)
+    def _():
+        part_copy().wait_send()
+        sum_copy().wait_recv()
+
+    @pl.when(c == 1)
+    def _():
         remote(p3, p3, small_send.at[1], small_recv.at[1], where(0)).wait()
         part[2] = part[1] + jnp.sum(p3[...], axis=0)
+
+        @pl.when(z < z_size - 1)
+        def _():
+            pl.semaphore_wait(column_sem, z_size - 1 - z)
+
         for k, device in column.items():
             remote(part.at[2], p2.at[k - 1], small_send.at[2], small_recv.at[2], device).start()
         remote(p2, p2, small_send.at[2], small_recv.at[2], column[1]).wait()
@@ -145,13 +193,35 @@
         k = early + lax.rem(i + turn, shards - early)
         return k, remote(nest.at[k], got.at[k], send_sem.at[k], recv_sem.at[k], where(k))
 
-    def send_nesterov(i, _):
+    def make_nesterov(i, _):
         k, copy = nesterov_copy(i)
         nest[k] = nesterov_of(pair_v[k, 0], m_v[index(k)])
-        copy.start()
-        return 0
-
-    lax.fori_loop(0, shards - early, send_nesterov, 0)
+
+        @pl.when(c * tail == 0)
+        def _():
+            copy.start()
+
+        return 0
+
+    def send_nesterov(i, _):
+        nesterov_copy(i)[1].start()
+        return 0
+
+    def nesterov_left(i, _):
+        nesterov_copy(i)[1].wait_send()
+        return 0
+
+    lax.fori_loop(0, shards - early, make_nesterov, 0)
+
+    @pl.when((1 - c) * tail > 0)
+    def _():
+        lax.fori_loop(0, tail - HOLD, nesterov_left, 0)
+        pl.semaphore_signal(go_sem, inc=1, device_id=other_core)
+
+    @pl.when(c * tail > 0)
+    def _():
+        pl.semaphore_wait(go_sem, 1)
+        lax.fori_loop(0, shards - early, send_nesterov, 0)
 
     def add_pair(k, total):
         remote(pair_v.at[k], got_pair.at[k], send_sem.at[k], pair_recv.at[k], where(k)).wait_recv()
@@ -226,15 +296,15 @@
         remote(pair_v.at[k], got_pair.at[k], send_sem.at[k], pair_recv.at[k], where(k)).wait_send()
         return 0
 
-    def nesterov_left(i, _):
-        nesterov_copy(i)[1].wait_send()
-        return 0
-
     lax.fori_loop(0, early, pair_left, 0)
-    lax.fori_loop(0, shards - early, nesterov_left, 0)
+
+    @pl.when((1 - c) * tail > 0)
+    def _():
+        lax.fori_loop(tail - HOLD, tail, nesterov_left, 0)
 
     @pl.when(c == 1)
     def _():
+        lax.fori_loop(0, shards - early, nesterov_left, 0)
         sum_copy().wait_send()
 
     remote(upd_ref, upd_ref, back_send, back_recv, where(0)).wait()
@@ -294,6 +364,10 @@
             dma,
             dma((5,)),
             dma((5,)),
+            pltpu.SemaphoreType.REGULAR,
+            pltpu.SemaphoreType.REGULAR,
+            pltpu.SemaphoreType.REGULAR,
+            pltpu.SemaphoreType.REGULAR,
         ],
         compiler_params=pltpu.CompilerParams(collective_id=0, has_side_effects=True, vmem_limit_bytes=24 << 20),
     )(*(pltpu.with_memory_space_constraint(a, pltpu.HBM) for a in arguments))

time: 62.3 us -> 61.8 us (level)
  no operation moved by 1% of the time
where the time goes in v3:
time: 61.8 us; the launch traced here: 61.7 us
  Pallas kernels  61 us (99%)
  between operations  0.64 us (1%)
    pallas_call x1, Pallas kernels, body(): pl.pallas_call(functools.partial(kernel, sizes, count), name='muon', out_...  59.6 us
    pallas_call x1, Pallas kernels, body(): pl.pallas_call(finish, name='finish', out_shape=tuple((jax.ShapeDtypeStru...  1.43 us

profile of v3, /device:TPU:1, one launch (start us, length us, event | category | flops | bytes accessed | tf_op | source)
XLA Modules:
  0.0 61.7 jit_solution(8268633227517592861)
XLA Ops:
  0.6 59.6 %muon.1 = (bf16[16,24,1024]{2,1,0:T(8,128)(2,1)S(1)}, f32[16,24,1024]{2,1,0:T(8,128)S(1)}, f32[1,1,2]{2,1,0:T(1,128)S(1)}) custom-call(bf16[16,24,1024]{2,1,0:T(8,128)(2,1)} %bitcast.6, f32[16,24,1024]{2,1,0:T(8,128)} %bitcast.5, s32[1,16]{1,0:T(1,128)} %bitcast.7), custom_call_target="tpu_custom_call" | custom-call | tf_op jit(solution)/shard_map/muon/pallas_call | solution.py:331
  60.2 1.4 %finish.1 = (bf16[16,24,1024]{2,1,0:T(8,128)(2,1)}, f32[16,24,1024]{2,1,0:T(8,128)}, f32[1,1,2]{2,1,0:T(1,128)}) custom-call(bf16[16,24,1024]{2,1,0:T(8,128)(2,1)S(1)} %get-tuple-element.9.refs_0_, f32[16,24,1024]{2,1,0:T(8,128)S(1)} %get-tuple-element.10.refs_1_, f32[1,1,2]{2,1,0:T(1,128)S(1)} %get-tuple-element.11.refs_2_), custom_call_target="tpu_custom_call" | custom-call | tf_op jit(solution)/shard_map/finish/pallas_call | solution.py:374

commit v4 on v3

--- a/solution.py
+++ b/solution.py
@@ -259,15 +259,20 @@
             product = lax.dot_general(gram_v[...], iterate, plain, preferred_element_type=jnp.float32)
             mat[...] = (QUINTIC_A * iterate.astype(jnp.float32) + product).astype(jnp.bfloat16)
 
-    chunk = 4 if shards % 4 == 0 else 2
+    chunk = yh_size
+    facing = 1 - 2 * yl
+    odd = lax.rem(x, 2)
+    columns = (0, 1, 3 - odd, 2 + odd)
     for i in range(shards // chunk):
-        first = lax.rem(i + turn, shards // chunk) * chunk
+        first = lax.rem((columns[i] - x) * facing + 2 * x_size, x_size) * chunk
         span = pl.ds(pl.multiple_of(first * rows, chunk * rows), chunk * rows)
         product = lax.dot_general(gram_v[span, :], mat[...], plain, preferred_element_type=jnp.float32)
         final = (QUINTIC_A * mat[span, :].astype(jnp.float32) + product) * math.sqrt(cols)
         for k in range(chunk):
             back[first + k] = final[k * rows:(k + 1) * rows].astype(jnp.bfloat16)
-            remote(back.at[first + k], upd_ref.at[me], back_send, back_recv, where(first + k)).start()
+        for there in sorted(range(yh_size), key=lambda h: min(h, yh_size - h)):
+            k = first + lax.rem((there - yh) * facing + 3 * yh_size - 1, yh_size)
+            remote(back.at[k], upd_ref.at[me], back_send, back_recv, where(k)).start()
 
     def keep(k, _):
         j = index(k)

time: 61.8 us -> 60.7 us (0.982)
  the two profiles are of different devices: /device:TPU:1 before, /device:TPU:13 now
where the time goes in v4:
time: 60.7 us; the launch traced here: 60.6 us
  Pallas kernels  59.9 us (99%)
  between operations  0.64 us (1%)
    pallas_call x1, Pallas kernels, body(): pl.pallas_call(functools.partial(kernel, sizes, count), name='muon', out_...  58.5 us
    pallas_call x1, Pallas kernels, body(): pl.pallas_call(finish, name='finish', out_shape=tuple((jax.ShapeDtypeStru...  1.43 us

profile of v4, /device:TPU:13, one launch (start us, length us, event | category | flops | bytes accessed | tf_op | source)
XLA Modules:
  0.0 60.6 jit_solution(14006035485367324448)
XLA Ops:
  0.6 58.5 %muon.1 = (bf16[16,24,1024]{2,1,0:T(8,128)(2,1)S(1)}, f32[16,24,1024]{2,1,0:T(8,128)S(1)}, f32[1,1,2]{2,1,0:T(1,128)S(1)}) custom-call(bf16[16,24,1024]{2,1,0:T(8,128)(2,1)} %bitcast.6, f32[16,24,1024]{2,1,0:T(8,128)} %bitcast.5, s32[1,16]{1,0:T(1,128)} %bitcast.7), custom_call_target="tpu_custom_call" | custom-call | tf_op jit(solution)/shard_map/muon/pallas_call | solution.py:336
  59.1 1.4 %finish.1 = (bf16[16,24,1024]{2,1,0:T(8,128)(2,1)}, f32[16,24,1024]{2,1,0:T(8,128)}, f32[1,1,2]{2,1,0:T(1,128)}) custom-call(bf16[16,24,1024]{2,1,0:T(8,128)(2,1)S(1)} %get-tuple-element.9.refs_0_, f32[16,24,1024]{2,1,0:T(8,128)S(1)} %get-tuple-element.10.refs_1_, f32[1,1,2]{2,1,0:T(1,128)S(1)} %get-tuple-element.11.refs_2_), custom_call_target="tpu_custom_call" | custom-call | tf_op jit(solution)/shard_map/finish/pallas_call | solution.py:379

commit v5 on v4

--- a/solution.py
+++ b/solution.py
@@ -223,36 +223,45 @@
         pl.semaphore_wait(go_sem, 1)
         lax.fori_loop(0, shards - early, send_nesterov, 0)
 
-    def add_pair(k, total):
-        remote(pair_v.at[k], got_pair.at[k], send_sem.at[k], pair_recv.at[k], where(k)).wait_recv()
-        block = nesterov_of(got_pair[k, 0], got_pair[k, 1])
-        got[k] = block
-        wide = block.astype(jnp.float32)
-        return total + wide * wide
-
-    def add_nesterov(k, total):
-        remote(nest.at[k], got.at[k], send_sem.at[k], recv_sem.at[k], where(k)).wait_recv()
-        wide = got[k].astype(jnp.float32)
-        return total + wide * wide
-
-    total = lax.fori_loop(early, shards, add_nesterov, lax.fori_loop(0, early, add_pair, nothing))
+    def keep_pair(i, blocks):
+        wide = jnp.concatenate(blocks, axis=0)
+        mat[pl.ds(pl.multiple_of(2 * i * rows, 2 * rows), 2 * rows), :] = wide.astype(jnp.bfloat16)
+        return blocks[0] * blocks[0] + blocks[1] * blocks[1]
+
+    def add_pair(i, total):
+        blocks = []
+        for k in (2 * i, 2 * i + 1):
+            remote(pair_v.at[k], got_pair.at[k], send_sem.at[k], pair_recv.at[k], where(k)).wait_recv()
+            blocks.append(nesterov_of(got_pair[k, 0], got_pair[k, 1]).astype(jnp.float32))
+        return total + keep_pair(i, blocks)
+
+    def add_nesterov(i, total):
+        blocks = []
+        for k in (2 * i, 2 * i + 1):
+            remote(nest.at[k], got.at[k], send_sem.at[k], recv_sem.at[k], where(k)).wait_recv()
+            blocks.append(got[k].astype(jnp.float32))
+        return total + keep_pair(i, blocks)
+
+    early_pairs = lax.div(early, 2)
+    total = lax.fori_loop(early_pairs, shards // 2, add_nesterov, lax.fori_loop(0, early_pairs, add_pair, nothing))
 
     norm = jnp.sqrt(jnp.full((1, LANES), jnp.sum(total), jnp.float32))
     scale = jnp.max(1.0 / (norm + 1e-07))
     square_row[...] = norm
     for k in range(shards):
         remote(square_row, squares.at[k], small_send.at[3], small_recv.at[3], where(k)).start()
-    for k in range(0, shards, 2):
-        pair = jnp.concatenate([got[k].astype(jnp.float32), got[k + 1].astype(jnp.float32)], axis=0)
-        mat[pl.ds(k * rows, 2 * rows), :] = (pair * scale).astype(jnp.bfloat16)
 
     over = (((1,), (1,)), ((), ()))
     plain = (((1,), (0,)), ((), ()))
     full = shards * rows
     for repeat in range(ITERS):
         iterate = mat[...]
-        gram_v[...] = lax.dot_general(iterate, iterate, over, preferred_element_type=jnp.float32).astype(jnp.bfloat16)
-        gram = gram_v[...]
+        product = lax.dot_general(iterate, iterate, over, preferred_element_type=jnp.float32)
+        if repeat == 0:
+            iterate = (iterate.astype(jnp.float32) * scale).astype(jnp.bfloat16)
+            product = product * scale * scale
+            mat[...] = iterate
+        gram = product.astype(jnp.bfloat16)
         squared_gram = lax.dot_general(gram, gram, plain, preferred_element_type=jnp.float32)
         gram_v[...] = (QUINTIC_B * gram.astype(jnp.float32) + QUINTIC_C * squared_gram).astype(jnp.bfloat16)
         if repeat < ITERS - 1:

time: 60.7 us -> 60.7 us (level)
  the two profiles are of different devices: /device:TPU:13 before, /device:TPU:21 now
where the time goes in v5:
time: 60.7 us; the launch traced here: 60.5 us
  Pallas kernels  59.9 us (99%)
  between operations  0.64 us (1%)
    pallas_call x1, Pallas kernels, body(): pl.pallas_call(functools.partial(kernel, sizes, count), name='muon', out_...  58.4 us
    pallas_call x1, Pallas kernels, body(): pl.pallas_call(finish, name='finish', out_shape=tuple((jax.ShapeDtypeStru...  1.43 us

profile of v5, /device:TPU:21, one launch (start us, length us, event | category | flops | bytes accessed | tf_op | source)
XLA Modules:
  0.0 60.5 jit_solution(5665673345861503788)
XLA Ops:
  0.6 58.4 %muon.1 = (bf16[16,24,1024]{2,1,0:T(8,128)(2,1)S(1)}, f32[16,24,1024]{2,1,0:T(8,128)S(1)}, f32[1,1,2]{2,1,0:T(1,128)S(1)}) custom-call(bf16[16,24,1024]{2,1,0:T(8,128)(2,1)} %bitcast.6, f32[16,24,1024]{2,1,0:T(8,128)} %bitcast.5, s32[1,16]{1,0:T(1,128)} %bitcast.7), custom_call_target="tpu_custom_call" | custom-call | tf_op jit(solution)/shard_map/muon/pallas_call | solution.py:345
  59.1 1.4 %finish.1 = (bf16[16,24,1024]{2,1,0:T(8,128)(2,1)}, f32[16,24,1024]{2,1,0:T(8,128)}, f32[1,1,2]{2,1,0:T(1,128)}) custom-call(bf16[16,24,1024]{2,1,0:T(8,128)(2,1)S(1)} %get-tuple-element.9.refs_0_, f32[16,24,1024]{2,1,0:T(8,128)S(1)} %get-tuple-element.10.refs_1_, f32[1,1,2]{2,1,0:T(1,128)S(1)} %get-tuple-element.11.refs_2_), custom_call_target="tpu_custom_call" | custom-call | tf_op jit(solution)/shard_map/finish/pallas_call | solution.py:388
